TPU v7x, 32 devices: a whole 2x2x4 slice. The times are simulated.
32 devices in a mesh: vc: 4 (over y, x), op: 8 (over z, core).
Axes of the slice: x: 2, y: 2, z: 4, core: 2. Of those that a mesh axis runs over, the one named last changes fastest.
Arguments:
- integrals: float32 [1024, 32768], P('op', 'vc'), may hold values from -0.046875 to 0.046875
- amplitudes: float32 [32768, 8192], P('vc', 'op'), may hold values from -6 to 6
- vir_energy: float32 [1024], P('vc'), may hold values from 1 to 10
- occ_energy: float32 [8192], P('op'), may hold values from -4 to -0.5
Outputs:
- update: float32 [1024, 8192], P('vc', 'op')
All inputs are finite; a program needn't handle non-finite values.
Results may differ from a plain program's by a relative error of at most 0.000076.
Values sent between devices are 32-bit elements; how exact they have to be, the bound alone decides.
No kernel may reach another device: no remote copies, remote signals or barrier semaphores. Data moves between devices by JAX's collectives and lax.ppermute only.
A program may use at most 128 MiB of HBM per device.

v0:
```python
import jax
import jax.numpy as jnp
from jax import lax
from jax.sharding import PartitionSpec as P


def shards(integrals, amplitudes, vir_energy, occ_energy):
    partial_sum = jnp.dot(
        lax.all_gather(integrals, "op", axis=0, tiled=True),
        amplitudes,
        precision=lax.Precision.HIGHEST,
        preferred_element_type=jnp.float32,
    )
    ladder = lax.psum_scatter(partial_sum, "vc", scatter_dimension=0, tiled=True)
    return ladder / (occ_energy[None, :] - vir_energy[:, None])


def solution(mesh):
    placed = (P("op", "vc"), P("vc", "op"), P("vc"), P("op"))
    return jax.shard_map(
        shards, mesh=mesh, in_specs=placed, out_specs=P("vc", "op"), check_vma=False
    )
```

profile of v0, /device:TPU:0, one launch (start us, length us, event | category | flops | bytes accessed | tf_op | source)
XLA Modules:
  0.0 475.0 jit_solution(10583772886767180605)
XLA Ops:
  6.5 0.0 all-gather.2.cloned.1.call-start
  6.5 0.7 all-gather.2.cloned.1.call-update
  7.3 0.0 copy-start
  7.3 0.0 copy-start.1
  7.3 0.0 reduce-scatter.2.cloned.1.call-start
  7.3 293.0 %all-gather.2.cloned.1.call-done = f32[1024,8192]{1,0:T(8,128)} async-done(((f32[128,8192]{1,0:T(8,128)}), f32[1024,8192]{1,0:T(8,128)}) %all-gather.2.cloned.1.call-update) | async-done | bytes 33554448 | tf_op jit(solution)/shard_map/all_gather | solution.py:9
  300.3 114.5 %fusion = f32[1024,1024]{1,0:T(8,128)} fusion(f32[1024,8192]{1,0:T(8,128)} %all-gather.2.cloned.1.call-done, f32[8192,1024]{1,0:T(8,128)} %param.5), kind=kOutput, calls=%fused_computation.1 | convolution fusion | flops 103079215104 | bytes 71303168 | tf_op jit(solution)/shard_map/dot_general | solution.py:8
  414.8 0.0 reduce-scatter.2.cloned.1.call-update
  414.8 50.9 %reduce-scatter.2.cloned.1.call-done = f32[256,1024]{1,0:T(8,128)} async-done(((f32[1024,1024]{1,0:T(8,128)}), f32[256,1024]{1,0:T(8,128)}) %reduce-scatter.2.cloned.1.call-update) | async-done | bytes 1048592 | tf_op jit(solution)/shard_map/reduce_scatter | solution.py:14
  465.7 0.0 copy-done
  465.7 0.0 copy-done.1
  465.7 2.4 subtract_divide_fusion
Async XLA Ops:
  6.5 293.8 %all-gather.2.cloned.1.call-start = ((), (), s32[]{:S(2)}) async-start(), calls=%async_computation.1 | async-start | bytes 37748736 | tf_op jit(solution)/shard_map/all_gather | solution.py:9
  7.3 458.5 %copy-start = (f32[1024]{0:T(1024)S(1)}, f32[1024]{0:T(1024)}, u32[]{:S(2)}) copy-start(f32[1024]{0:T(1024)} %param.7) | copy-start | bytes 12292
  7.3 458.5 %copy-start.1 = (f32[256]{0:T(256)S(1)}, f32[256]{0:T(256)}, u32[]{:S(2)}) copy-start(f32[256]{0:T(256)} %param.6) | copy-start | bytes 3076
  7.3 458.5 %reduce-scatter.2.cloned.1.call-start = ((), (), s32[]{:S(2)}) async-start(), calls=%async_computation.2 | async-start | bytes 5242880 | tf_op jit(solution)/shard_map/reduce_scatter | solution.py:14
Sparse Core Ops, SparseCore 0:
  8.9 291.3 all-gather.1
  414.9 50.7 reduce-scatter.1
where the time goes:
time: 475 us
  waiting for transfers between devices  345 us (73%)
  matrix products  114 us (24%)
  between operations  13.4 us (3%)
    all_gather x1, waiting for transfers between devices, shards(): lax.all_gather(integrals, 'op', axis=0, tiled=True)  293 us
    dot_general x1, matrix products, shards(): jnp.dot(lax.all_gather(integrals, 'op', axis=0, tiled=True), amplitudes,...  114 us
    reduce_scatter x1, waiting for transfers between devices, shards(): lax.psum_scatter(partial_sum, 'vc', scatter_dimension=0, tiled=True)  50.9 us
  transfers between devices with their start and end apart: 2, of which 2 were waited for; matrix products, arithmetic and copies ran while one was open for 0% of the time, Pallas kernels for 0%

commit v1 on v0

v1 whole, which is shorter than its diff:
```python
import jax
import jax.numpy as jnp
from jax import lax
from jax.sharding import PartitionSpec as P

CHUNKS = 4


def solution(mesh):
    vc, op = mesh.shape["vc"], mesh.shape["op"]

    def shards(integrals, amplitudes, vir_energy, occ_energy):
        rows = integrals.shape[0] // CHUNKS
        cols = amplitudes.shape[1]
        pieces = []
        for c in range(CHUNKS):
            part = lax.slice_in_dim(integrals, c * rows, (c + 1) * rows, axis=0)
            whole = lax.all_gather(part, "op", axis=0, tiled=True)
            partial_sum = jnp.dot(
                whole,
                amplitudes,
                precision=lax.Precision.HIGH,
                preferred_element_type=jnp.float32,
            )
            mine = lax.psum_scatter(partial_sum, "vc", scatter_dimension=0, tiled=True)
            pieces.append(mine.reshape(op // vc, rows, cols))
        ladder = jnp.concatenate(pieces, axis=1).reshape(-1, cols)
        return ladder / (occ_energy[None, :] - vir_energy[:, None])

    placed = (P("op", "vc"), P("vc", "op"), P("vc"), P("op"))
    return jax.shard_map(
        shards, mesh=mesh, in_specs=placed, out_specs=P("vc", "op"), check_vma=False
    )
```

time: 475 us -> 473 us (level)
  matrix products: 114 us -> 88.4 us
  waiting for transfers between devices: 345 us -> 364 us
    reduce_scatter x1 -> x4, waiting for transfers between devices: 50.9 us -> 99.5 us  [shards(): mine = lax.psum_scatter(partial_sum, 'vc', scatter_dimension=0, tiled=True)]
    all_gather x1 -> x4, waiting for transfers between devices: 293 us -> 262 us  [shards(): whole = lax.all_gather(part, 'op', axis=0, tiled=True)]
    dot_general x1 -> x4, matrix products: 114 us -> 88.4 us  [shards(): jnp.dot(whole, amplitudes, precision=lax.Precision.HIGH, preferred_elemen...]
  transfers between devices with their start and end apart: 2 -> 8, of which waited for: 2 -> 8; matrix products, arithmetic and copies ran while one was open for 0% -> 19% of each run, Pallas kernels for 0% -> 0%
where the time goes in v1:
time: 473 us
  waiting for transfers between devices  364 us (77%)
  matrix products  88.4 us (19%)
  between operations  13.5 us (3%)
    all_gather x4, waiting for transfers between devices, shards(): whole = lax.all_gather(part, 'op', axis=0, tiled=True)  262 us
    reduce_scatter x4, waiting for transfers between devices, shards(): mine = lax.psum_scatter(partial_sum, 'vc', scatter_dimension=0, tiled=True)  99.5 us
    dot_general x4, matrix products, shards(): jnp.dot(whole, amplitudes, precision=lax.Precision.HIGH, preferred_elemen...  88.4 us
  transfers between devices with their start and end apart: 8, of which 8 were waited for; matrix products, arithmetic and copies ran while one was open for 19% of the time, Pallas kernels for 0%

profile of v1, /device:TPU:0, one launch (start us, length us, event | category | flops | bytes accessed | tf_op | source)
XLA Modules:
  0.0 473.0 jit_solution(10531098516815276707)
XLA Ops:
  6.5 0.0 all-gather.5.cloned.1.call-start
  6.5 4.3 fusion
  10.8 0.0 all-gather.5.cloned.1.call-update
  10.8 0.0 all-gather.7.cloned.1.call-start
  10.9 0.7 all-gather.7.cloned.1.call-update
  11.6 0.0 all-gather.11.cloned.1.call-start
  11.6 0.7 all-gather.11.cloned.1.call-update
  12.3 0.0 all-gather.9.cloned.1.call-start
  12.4 0.5 all-gather.9.cloned.1.call-update
  12.9 0.0 reduce-scatter.5.cloned.1.call-start
  12.9 82.8 %all-gather.5.cloned.1.call-done = f32[256,8192]{1,0:T(8,128)} async-done(((f32[32,8192]{1,0:T(8,128)}), f32[256,8192]{1,0:T(8,128)}) %all-gather.5.cloned.1.call-update) | async-done | bytes 8388624 | tf_op jit(solution)/shard_map/all_gather | solution.py:18
  95.7 22.1 %fusion.1 = f32[256,1024]{1,0:T(8,128)} fusion(f32[256,8192]{1,0:T(8,128)} %all-gather.5.cloned.1.call-done, f32[8192,1024]{1,0:T(8,128)} %param.5), kind=kOutput, calls=%fused_computation.3 | convolution fusion | flops 12884901888 | bytes 42991616 | tf_op jit(solution)/shard_map/dot_general | solution.py:19
  117.8 0.0 reduce-scatter.5.cloned.1.call-update
  117.9 0.0 reduce-scatter.7.cloned.1.call-start
  117.9 60.0 %all-gather.7.cloned.1.call-done = f32[256,8192]{1,0:T(8,128)} async-done(((f32[32,8192]{1,0:T(8,128)}), f32[256,8192]{1,0:T(8,128)}) %all-gather.7.cloned.1.call-update) | async-done | bytes 8388624 | tf_op jit(solution)/shard_map/all_gather | solution.py:18
  177.9 22.2 %fusion.2 = f32[256,1024]{1,0:T(8,128)} fusion(f32[256,8192]{1,0:T(8,128)} %all-gather.7.cloned.1.call-done, f32[8192,1024]{1,0:T(8,128)} %param.5), kind=kOutput, calls=%fused_computation.4 | convolution fusion | flops 12884901888 | bytes 42991616 | tf_op jit(solution)/shard_map/dot_general | solution.py:19
  200.1 0.0 reduce-scatter.7.cloned.1.call-update
  200.1 0.2 reduce-scatter.11.cloned.1.call-start
  200.3 59.7 %all-gather.11.cloned.1.call-done = f32[256,8192]{1,0:T(8,128)} async-done(((f32[32,8192]{1,0:T(8,128)}), f32[256,8192]{1,0:T(8,128)}) %all-gather.11.cloned.1.call-update) | async-done | bytes 8388624 | tf_op jit(solution)/shard_map/all_gather | solution.py:18
  260.1 22.1 %fusion.4 = f32[256,1024]{1,0:T(8,128)} fusion(f32[256,8192]{1,0:T(8,128)} %all-gather.11.cloned.1.call-done, f32[8192,1024]{1,0:T(8,128)} %param.5), kind=kOutput, calls=%fused_computation.6 | convolution fusion | flops 12884901888 | bytes 42991616 | tf_op jit(solution)/shard_map/dot_general | solution.py:19
  282.1 0.0 reduce-scatter.11.cloned.1.call-update
  282.2 0.0 copy-start
  282.2 0.0 copy-start.1
  282.2 0.0 reduce-scatter.9.cloned.1.call-start
  282.2 59.8 %all-gather.9.cloned.1.call-done = f32[256,8192]{1,0:T(8,128)} async-done(((f32[32,8192]{1,0:T(8,128)}), f32[256,8192]{1,0:T(8,128)}) %all-gather.9.cloned.1.call-update) | async-done | bytes 8388624 | tf_op jit(solution)/shard_map/all_gather | solution.py:18
  342.1 22.1 %fusion.3 = f32[256,1024]{1,0:T(8,128)} fusion(f32[256,8192]{1,0:T(8,128)} %all-gather.9.cloned.1.call-done, f32[8192,1024]{1,0:T(8,128)} %param.5), kind=kOutput, calls=%fused_computation.5 | convolution fusion | flops 12884901888 | bytes 42991616 | tf_op jit(solution)/shard_map/dot_general | solution.py:19
  364.1 0.0 reduce-scatter.9.cloned.1.call-update
  364.2 7.1 %reduce-scatter.5.cloned.1.call-done = f32[64,1024]{1,0:T(8,128)} async-done(((f32[256,1024]{1,0:T(8,128)}), f32[64,1024]{1,0:T(8,128)}) %reduce-scatter.5.cloned.1.call-update) | async-done | bytes 262160 | tf_op jit(solution)/shard_map/reduce_scatter | solution.py:25
  371.3 30.7 %reduce-scatter.7.cloned.1.call-done = f32[64,1024]{1,0:T(8,128)} async-done(((f32[256,1024]{1,0:T(8,128)}), f32[64,1024]{1,0:T(8,128)}) %reduce-scatter.7.cloned.1.call-update) | async-done | bytes 262160 | tf_op jit(solution)/shard_map/reduce_scatter | solution.py:25
  402.0 30.9 %reduce-scatter.11.cloned.1.call-done = f32[64,1024]{1,0:T(8,128)} async-done(((f32[256,1024]{1,0:T(8,128)}), f32[64,1024]{1,0:T(8,128)}) %reduce-scatter.11.cloned.1.call-update) | async-done | bytes 262160 | tf_op jit(solution)/shard_map/reduce_scatter | solution.py:25
  432.8 30.9 %reduce-scatter.9.cloned.1.call-done = f32[64,1024]{1,0:T(8,128)} async-done(((f32[256,1024]{1,0:T(8,128)}), f32[64,1024]{1,0:T(8,128)}) %reduce-scatter.9.cloned.1.call-update) | async-done | bytes 262160 | tf_op jit(solution)/shard_map/reduce_scatter | solution.py:25
  463.7 1.3 pad_maximum_fusion
  465.0 0.0 copy-done
  465.0 0.0 copy-done.1
  465.0 1.2 bitcast_divide_fusion
Async XLA Ops:
  6.5 89.2 %all-gather.5.cloned.1.call-start = ((), (), s32[]{:S(2)}) async-start(), calls=%async_computation.4 | async-start | bytes 9437184 | tf_op jit(solution)/shard_map/all_gather | solution.py:18
  10.8 167.1 %all-gather.7.cloned.1.call-start = ((), (), s32[]{:S(2)}) async-start(), calls=%async_computation.6 | async-start | bytes 9437184 | tf_op jit(solution)/shard_map/all_gather | solution.py:18
  11.6 248.5 %all-gather.11.cloned.1.call-start = ((), (), s32[]{:S(2)}) async-start(), calls=%async_computation.10 | async-start | bytes 9437184 | tf_op jit(solution)/shard_map/all_gather | solution.py:18
  12.3 329.7 %all-gather.9.cloned.1.call-start = ((), (), s32[]{:S(2)}) async-start(), calls=%async_computation.8 | async-start | bytes 9437184 | tf_op jit(solution)/shard_map/all_gather | solution.py:18
  12.9 358.4 %reduce-scatter.5.cloned.1.call-start = ((), (), s32[]{:S(2)}) async-start(), calls=%async_computation.5 | async-start | bytes 1310720 | tf_op jit(solution)/shard_map/reduce_scatter | solution.py:25
  117.9 284.1 %reduce-scatter.7.cloned.1.call-start = ((), (), s32[]{:S(2)}) async-start(), calls=%async_computation.7 | async-start | bytes 1310720 | tf_op jit(solution)/shard_map/reduce_scatter | solution.py:25
  200.1 232.7 %reduce-scatter.11.cloned.1.call-start = ((), (), s32[]{:S(2)}) async-start(), calls=%async_computation.11 | async-start | bytes 1310720 | tf_op jit(solution)/shard_map/reduce_scatter | solution.py:25
  282.2 182.8 %copy-start = (f32[1024]{0:T(1024)S(1)}, f32[1024]{0:T(1024)}, u32[]{:S(2)}) copy-start(f32[1024]{0:T(1024)} %param.7) | copy-start | bytes 12292
  282.2 182.8 %copy-start.1 = (f32[256]{0:T(256)S(1)}, f32[256]{0:T(256)}, u32[]{:S(2)}) copy-start(f32[256]{0:T(256)} %param.6) | copy-start | bytes 3076
  282.2 181.5 %reduce-scatter.9.cloned.1.call-start = ((), (), s32[]{:S(2)}) async-start(), calls=%async_computation.9 | async-start | bytes 1310720 | tf_op jit(solution)/shard_map/reduce_scatter | solution.py:25
Sparse Core Ops, SparseCore 0:
  10.9 84.7 all-gather.4
  97.3 80.5 all-gather.6
  179.5 80.5 all-gather.10
  261.5 80.5 all-gather.8
  344.8 26.4 reduce-scatter.4
  374.0 27.9 reduce-scatter.6
  404.8 27.9 reduce-scatter.10
  435.7 27.9 reduce-scatter.8
